TPU v7x, 32 devices: a whole 2x2x4 slice. The times are simulated.
32 devices in a mesh: gx: 8 (over z, y), gy: 4 (over x, core).
Axes of the slice: x: 2, y: 2, z: 4, core: 2. Of those that a mesh axis runs over, the one named last changes fastest.
Arguments:
- scalar: float32 [2, 512, 8, 4, 128], P(None, None, 'gx', 'gy'), may hold values from -6 to 6
- velocity: float32 [3, 2, 512, 8, 4, 128], P(None, None, None, 'gx', 'gy'), may hold values from -1 to 1
- diffusivity: float32 [2, 8, 4, 128], P(None, 'gx', 'gy'), may hold values from 0.005 to 0.05
- recv_owner: int32 [65536, 1], P(('gx', 'gy')), may hold values from 0 to 31; in each aligned block of 2048 rows (0 to 2047, 2048 to 4095, ...) at most 128 rows name the same one
- donor_elem: int32 [65536], P(('gx', 'gy')), may hold values from 0 to 127
- recv_point: int32 [65536], P(('gx', 'gy')), may hold values from 0 to 65535
- recv_coords: float32 [3, 65536], P(None, ('gx', 'gy')), may hold values from -1 to 1
Outputs:
- advanced: float32 [2, 512, 8, 4, 128], P(None, None, 'gx', 'gy')
Inputs may be any that keep to these rules, and one draw needn't show every extreme that they name: `recv_owner`: among the 2048 receivers of one device no owner is named more than 128 times, a bound that some block reaches.
All inputs are finite; a program needn't handle non-finite values.
Results may differ from a plain program's by a relative error of at most 0.0003.
Values sent between devices are 32-bit elements; how exact they have to be, the bound alone decides.
A program may use at most 128 MiB of HBM per device.

v0:
```python
import functools
import jax
import jax.numpy as jnp
import numpy as np
from jax import lax
from jax.experimental import pallas as pl
from jax.experimental.pallas import tpu as pltpu
from jax.sharding import PartitionSpec as P

time_step = 0.01
penalty_rate = 50.0
metric = 2.0
volume_factor = 0.125
node_inner = [0.8717401485096066, 0.5917001814331423, 0.20929921790247888]


def legendre_seven(point):
    before, current = (1.0, point)
    for order in range(1, 7):
        before, current = (
            current,
            ((2 * order + 1) * point * current - order * before) / (order + 1),
        )
    return current


def gll_tables():
    degree = 7
    gll_nodes = [
        -1.0,
        -node_inner[0],
        -node_inner[1],
        -node_inner[2],
        node_inner[2],
        node_inner[1],
        node_inner[0],
        1.0,
    ]
    end_values = [legendre_seven(v) for v in gll_nodes]
    weights = [2.0 / (degree * (degree + 1) * v * v) for v in end_values]
    derivative = [[0.0] * 8 for _ in range(8)]
    for a in range(8):
        for b in range(8):
            if a != b:
                derivative[a][b] = end_values[a] / (end_values[b] * (gll_nodes[a] - gll_nodes[b]))
    derivative[0][0] = -degree * (degree + 1) / 4.0
    derivative[7][7] = degree * (degree + 1) / 4.0
    weight_row = jnp.asarray(weights, jnp.float32)
    cube_weights = weight_row[:, None, None] * weight_row[None, :, None] * weight_row[None, None, :]
    return (gll_nodes, cube_weights, derivative)


MESH = pl.DeviceIdType.MESH
HEADINGS = [(-1, 0), (1, 0), (0, -1), (0, 1), (-1, -1), (-1, 1), (1, -1), (1, 1)]


def halves(value):
    high = value.astype(jnp.bfloat16)
    return high, (value - high.astype(jnp.float32)).astype(jnp.bfloat16)


def mm(a, b):
    return jnp.dot(a, b, preferred_element_type=jnp.float32)


def mm_t(a, b):
    return lax.dot_general(a, b, (((1,), (1,)), ((), ())), preferred_element_type=jnp.float32)


def mm3(op_high, op_low, value):
    high, low = halves(value)
    return mm(op_high, high) + mm(op_high, low) + mm(op_low, high)


def step_kernel(
    derivative, gll_nodes, start_ref, vel_ref, nu_ref, wm_ref, dim_ref, ops_ref, asked_ref, slot_q_ref, slot_e_ref,
    out_ref,
    cur, local, work, grad, pick, spread_q, spread_e, count, ans, rep, hx, hy, he, got, basis_ref,
    ask_send, ask_recv,
    ans_send, ans_recv, halo_send, halo_recv,
):
    gx, gy = lax.axis_index("gx"), lax.axis_index("gy")
    nx, ny = lax.axis_size("gx"), lax.axis_size("gy")
    n = nx * ny
    me = gx * ny + gy
    ez = start_ref.shape[-1]
    groups, _, lanes = slot_q_ref.shape
    cap = ans.shape[-1]
    per = lanes // cap

    barrier = pltpu.get_barrier_semaphore()

    def greet(step, carry):
        d = lax.rem(me + step, n)
        pl.semaphore_signal(barrier, inc=1, device_id=(d // ny, lax.rem(d, ny)), device_id_type=MESH)
        return carry

    hx[...] = jnp.zeros_like(hx)
    hy[...] = jnp.zeros_like(hy)
    he[...] = jnp.zeros_like(he)
    lax.fori_loop(1, n, greet, 0)

    pl.semaphore_wait(barrier, n - 1)

    def ask(step, carry):
        d = lax.rem(me + step, n)
        pltpu.make_async_remote_copy(
            src_ref=asked_ref.at[d], dst_ref=got.at[me], send_sem=ask_send, recv_sem=ask_recv,
            device_id=(d // ny, lax.rem(d, ny)), device_id_type=MESH,
        ).start()
        return carry

    lax.fori_loop(1, n, ask, 0)
    count[...] = jnp.zeros_like(count)

    def build(g, carry):
        wide = lax.broadcasted_iota(jnp.int32, (2 * ez, lanes), 0)
        tall = lax.broadcasted_iota(jnp.int32, (512, lanes), 0)
        spread_e[g] = jnp.where(wide == slot_e_ref[g], 1.0, 0.0).astype(jnp.bfloat16)
        spread_q[g] = jnp.where(tall == slot_q_ref[g], 1.0, 0.0).astype(jnp.bfloat16)
        count[...] += mm_t(spread_q[g], spread_e[g])
        return carry

    lax.fori_loop(0, groups, build, 0)
    cur[...] = start_ref[...]
    got[me] = asked_ref[me]
    first = got.at[pl.ds(0, n - 1)]
    pltpu.make_async_copy(first, first, ask_recv).wait()

    def prepare(g, carry):
        asked = jnp.concatenate([got[g * per + t] for t in range(per)], axis=1)
        wide = lax.broadcasted_iota(jnp.int32, (2 * ez, lanes), 0)
        pick[g] = jnp.where(wide == asked[3:4].astype(jnp.int32), 1.0, 0.0).astype(jnp.bfloat16)
        for j in range(8):
            factor = jnp.ones_like(asked)
            for k in range(8):
                if k != j:
                    factor = factor * ((asked - gll_nodes[k]) * (1.0 / (gll_nodes[j] - gll_nodes[k])))
            for c in range(3):
                basis_ref[g, 8 * c + j:8 * c + j + 1, :] = factor[c:c + 1]
        return carry

    lax.fori_loop(0, groups, prepare, 0)

    def halo_copy(s, number):
        dx, dy = HEADINGS[number]
        rows = pl.ds(0 if dy < 0 else 56, 8)
        plane = 0 if dx < 0 else 7
        if dy == 0:
            source, target = local.at[:, plane], hx.at[s, number]
        elif dx == 0:
            source, target = local.at[:, :, rows, :], hy.at[s, number - 2]
        else:
            source, target = local.at[:, plane, rows, :], he.at[s, number - 4]
        return pltpu.make_async_remote_copy(
            src_ref=source, dst_ref=target, send_sem=halo_send.at[s, number], recv_sem=halo_recv.at[s, number],
            device_id=(gx + dx, gy + dy), device_id_type=MESH,
        )

    def inside(dx, dy):
        return (gx + dx >= 0) & (gx + dx < nx) & (gy + dy >= 0) & (gy + dy < ny)

    for s in range(3):
        both = jnp.concatenate([cur[0].reshape(512, ez), cur[1].reshape(512, ez)], axis=1)
        high, low = halves(both)

        def interpolate(g, carry):
            found = mm(high, pick[g]) + mm(low, pick[g])
            acc = found[0:64] * basis_ref[g, 0:1, :]
            for i in range(1, 8):
                acc = acc + found[64 * i:64 * i + 64] * basis_ref[g, i:i + 1, :]
            acc2 = acc[0:8] * basis_ref[g, 8:9, :]
            for j in range(1, 8):
                acc2 = acc2 + acc[8 * j:8 * j + 8] * basis_ref[g, 8 + j:9 + j, :]
            row = jnp.sum(acc2 * basis_ref[g, 16:24, :], axis=0, keepdims=True)
            for t in range(per):
                ans[s, g * per + t] = row[:, t * cap:(t + 1) * cap]
            return carry

        lax.fori_loop(0, groups, interpolate, 0)

        def send(step, carry):
            d = lax.rem(me + step, n)
            pltpu.make_async_remote_copy(
                src_ref=ans.at[s, d], dst_ref=rep.at[s, me], send_sem=ans_send.at[s], recv_sem=ans_recv.at[s],
                device_id=(d // ny, lax.rem(d, ny)), device_id_type=MESH,
            ).start()
            return carry

        lax.fori_loop(1, n, send, 0)

        for m in range(2):
            lo_lane = m * ez
            scale = nu_ref[m:m + 1, :]
            for half in range(2):
                part = cur[m, 4 * half:4 * half + 4].reshape(256, ez)
                grad[0, 4 * half:4 * half + 4, :, lo_lane:lo_lane + ez] = mm3(ops_ref[0], ops_ref[1], part).reshape(4, 64, ez)
                grad[1, 4 * half:4 * half + 4, :, lo_lane:lo_lane + ez] = mm3(ops_ref[2], ops_ref[3], part).reshape(4, 64, ez)
            for a in range(8):
                gxa = (2.0 * derivative[a][0]) * cur[m, 0]
                for i in range(1, 8):
                    gxa = gxa + (2.0 * derivative[a][i]) * cur[m, i]
                wm = wm_ref[a]
                gya = grad[0, a, :, lo_lane:lo_lane + ez]
                gza = grad[1, a, :, lo_lane:lo_lane + ez]
                adv = vel_ref[0, m, a] * gxa + vel_ref[1, m, a] * gya + vel_ref[2, m, a] * gza
                local[m, a] = -(wm * adv)
                wn = wm * scale
                work[m, a] = wn * gxa
                grad[0, a, :, lo_lane:lo_lane + ez] = wn * gya
                grad[1, a, :, lo_lane:lo_lane + ez] = wn * gza
            for half in range(2):
                part_y = grad[0, 4 * half:4 * half + 4, :, lo_lane:lo_lane + ez].reshape(256, ez)
                part_z = grad[1, 4 * half:4 * half + 4, :, lo_lane:lo_lane + ez].reshape(256, ez)
                back = mm3(ops_ref[4], ops_ref[5], part_y) + mm3(ops_ref[6], ops_ref[7], part_z)
                local[m, 4 * half:4 * half + 4] -= back.reshape(4, 64, ez)
            for i in range(8):
                total = (2.0 * derivative[0][i]) * work[m, 0]
                for a in range(1, 8):
                    total = total + (2.0 * derivative[a][i]) * work[m, a]
                local[m, i] -= total

        rep[s, me] = ans[s, me]
        whole = rep.at[s, pl.ds(0, n - 1)]
        pltpu.make_async_copy(whole, whole, ans_recv.at[s]).wait()

        work[...] = jnp.zeros_like(work)

        def scatter(g, carry):
            row = jnp.concatenate([rep[s, g * per + t] for t in range(per)], axis=1)
            row_high, row_low = halves(row)
            where_e = spread_e[g]
            added = mm_t(spread_q[g], where_e * row_high) + mm_t(spread_q[g], where_e * row_low)
            work[0] += added[:, :ez].reshape(8, 64, ez)
            work[1] += added[:, ez:].reshape(8, 64, ez)
            return carry

        lax.fori_loop(0, groups, scatter, 0)
        for m in range(2):
            for i in range(8):
                held = count[64 * i:64 * i + 64, m * ez:(m + 1) * ez]
                local[m, i] += penalty_rate * wm_ref[i] * (work[m, i] - held * cur[m, i])

        for number, (dx, dy) in enumerate(HEADINGS):
            @pl.when(inside(dx, dy))
            def _(number=number):
                halo_copy(s, number).start()

        for number, (dx, dy) in enumerate(HEADINGS):
            @pl.when(inside(-dx, -dy))
            def _(number=number):
                halo_copy(s, number).wait_recv()

        work[...] = local[...]
        for m in range(2):
            work[m, 7] += hx[s, 0, m]
            work[m, 0] += hx[s, 1, m]
            work[m, :, 56:64, :] += hy[s, 0, m]
            work[m, :, 0:8, :] += hy[s, 1, m]
            work[m, 7, 56:64, :] += he[s, 0, m]
            work[m, 7, 0:8, :] += he[s, 1, m]
            work[m, 0, 56:64, :] += he[s, 2, m]
            work[m, 0, 0:8, :] += he[s, 3, m]

        for m in range(2):
            flat = work[m].reshape(512, ez)
            depth = lax.rem(lax.broadcasted_iota(jnp.int32, (512, ez), 0), 8)
            lane = lax.broadcasted_iota(jnp.int32, (512, ez), 1)
            after = pltpu.roll(pltpu.roll(flat, 7, 0), ez - 1, 1)
            before = pltpu.roll(pltpu.roll(flat, 505, 0), 1, 1)
            flat = flat + jnp.where((depth == 7) & (lane < ez - 1), after, 0.0)
            flat = flat + jnp.where((depth == 0) & (lane > 0), before, 0.0)
            moved = cur[m] + flat.reshape(8, 64, ez) * dim_ref[...]
            if s == 0:
                cur[m] = moved
            elif s == 1:
                cur[m] = 0.75 * start_ref[m] + 0.25 * moved
            else:
                out_ref[m] = 2.0 / 3.0 * moved

        for number, (dx, dy) in enumerate(HEADINGS):
            @pl.when(inside(dx, dy))
            def _(number=number):
                halo_copy(s, number).wait_send()

    sent = got.at[pl.ds(0, n - 1)]
    pltpu.make_async_copy(sent, sent, ask_send).wait()
    for s in range(3):
        whole = ans.at[s, pl.ds(0, n - 1)]
        pltpu.make_async_copy(whole, whole, ans_send.at[s]).wait()


def split_host(matrix):
    high = matrix.astype(jnp.bfloat16)
    low = (matrix - high.astype(np.float64)).astype(jnp.bfloat16)
    return [high, low]


def body(scalar, velocity, diffusivity, recv_owner, donor_elem, recv_point, recv_coords):
    gll_nodes, cube_weights, derivative = gll_tables()
    ez = scalar.shape[4]
    elems = scalar.shape[2] * scalar.shape[3] * ez
    width_x, width_y = lax.axis_size("gx"), lax.axis_size("gy")
    n = width_x * width_y
    rows = recv_owner.shape[0]
    cap = max(2, 2 * rows // n)
    slots_all = n * cap
    per = max(1, min(n, 512 // cap))
    groups, lanes = n // per, per * cap

    owners = recv_owner[:, 0]
    bf, f32 = jnp.bfloat16, jnp.float32
    hot = (owners[None, :] == jnp.arange(n, dtype=jnp.int32)[:, None]).astype(bf)
    width = min(256, rows)
    blocks = rows // width
    earlier = jnp.asarray(np.triu(np.ones((width, width)), 1), bf)
    hot3 = hot.reshape(n, blocks, width)
    within = jnp.einsum("nbr,rs->nbs", hot3, earlier, preferred_element_type=f32)
    sums = jnp.sum(hot3.astype(f32), axis=2)
    strict = np.triu(np.ones((blocks, blocks)), 1).astype(np.float32)
    offset = jnp.sum(sums[:, :, None] * strict[None], axis=1)
    rank = jnp.sum((within + offset[:, :, None]) * hot3.astype(f32), axis=0).reshape(rows)
    slot_hot = (rank[None, :].astype(jnp.int32) == jnp.arange(cap, dtype=jnp.int32)[:, None]).astype(bf)

    own_mesh = (jnp.arange(rows, dtype=jnp.int32) >= rows // 2).astype(jnp.int32)
    point_q, point_e = recv_point // elems, recv_point % elems
    high = lax.reduce_precision(recv_coords, 8, 7)
    middle = lax.reduce_precision(recv_coords - high, 8, 7)
    low = recv_coords - high - middle
    ints = jnp.stack([donor_elem, 1 - own_mesh, point_q // 8 + 1, point_q % 8, point_e, own_mesh]).astype(f32)
    data = jnp.concatenate([high, middle, low, ints], axis=0).astype(bf)
    routed = jnp.einsum("cnr,kr->nck", data[:, None, :] * hot[None], slot_hot, preferred_element_type=f32)
    coords = routed[:, 0:3] + routed[:, 3:6] + routed[:, 6:9]
    asked = jnp.concatenate([coords, routed[:, 9:10] + elems * routed[:, 10:11]], axis=1)
    def grouped(piece):
        return piece.astype(jnp.int32).reshape(groups, 1, lanes)

    slot_q = grouped((routed[:, 11] - 1.0) * 8.0 + routed[:, 12])
    slot_e = grouped(routed[:, 13] + elems * routed[:, 14])
    half_eye = np.eye(4)
    table = 2.0 * np.asarray(derivative, np.float64)
    along_y = np.kron(half_eye, np.kron(table, np.eye(8)))
    along_z = np.kron(half_eye, np.kron(np.eye(8), table))
    ops = []
    for matrix in (along_y, along_z, along_y.T, along_z.T):
        ops = ops + split_host(matrix)
    ops = jnp.asarray(np.stack(ops))

    weights = np.asarray([2.0 / (56.0 * legendre_seven(v) ** 2) for v in gll_nodes], np.float64)
    shared = jnp.asarray(weights + weights[::-1] * (np.arange(8) % 7 == 0), f32)
    single = jnp.asarray(weights, f32)
    ends = jnp.arange(8)

    def line_mass(position, count):
        joined = ((ends == 0) & (position > 0)) | ((ends == 7) & (position < count - 1))
        return jnp.where(joined, shared, single)

    mass_x = line_mass(lax.axis_index("gx"), width_x)
    mass_y = line_mass(lax.axis_index("gy"), width_y)
    place = jnp.arange(ez)[None, :]
    joined_z = ((ends[:, None] == 0) & (place > 0)) | ((ends[:, None] == 7) & (place < ez - 1))
    mass_z = jnp.where(joined_z, shared[:, None], single[:, None])
    mass = volume_factor * mass_x[:, None, None, None] * mass_y[None, :, None, None] * mass_z[None, None]
    step_mass = (time_step / mass).reshape(8, 64, ez)
    wm = jnp.broadcast_to((volume_factor * cube_weights).reshape(8, 64, 1), (8, 64, ez))

    vmem = pltpu.VMEM
    out = pl.pallas_call(
        functools.partial(step_kernel, derivative, gll_nodes),
        out_shape=jax.ShapeDtypeStruct((2, 8, 64, ez), f32),
        in_specs=[pl.BlockSpec(memory_space=vmem)] * 9,
        out_specs=pl.BlockSpec(memory_space=vmem),
        scratch_shapes=[
            vmem((2, 8, 64, ez), f32),
            vmem((2, 8, 64, ez), f32),
            vmem((2, 8, 64, ez), f32),
            vmem((2, 8, 64, 2 * ez), f32),
            vmem((groups, 2 * ez, lanes), bf),
            vmem((groups, 512, lanes), bf),
            vmem((groups, 2 * ez, lanes), bf),
            vmem((512, 2 * ez), f32),
            vmem((3, n, 1, cap), f32),
            vmem((3, n, 1, cap), f32),
            vmem((3, 2, 2, 64, ez), f32),
            vmem((3, 2, 2, 8, 8, ez), f32),
            vmem((3, 4, 2, 8, ez), f32),
            vmem((n, 4, cap), f32),
            vmem((groups, 24, lanes), f32),
            pltpu.SemaphoreType.DMA,
            pltpu.SemaphoreType.DMA,
            pltpu.SemaphoreType.DMA((3,)),
            pltpu.SemaphoreType.DMA((3,)),
            pltpu.SemaphoreType.DMA((3, 8)),
            pltpu.SemaphoreType.DMA((3, 8)),
        ],
        compiler_params=pltpu.CompilerParams(collective_id=0, has_side_effects=True),
        name="advance",
    )(
        scalar.reshape(2, 8, 64, ez), velocity.reshape(3, 2, 8, 64, ez), diffusivity.reshape(2, ez),
        wm, step_mass, ops, asked, slot_q, slot_e,
    )
    return scalar / 3.0 + out.reshape(scalar.shape)


def solution(mesh):
    return jax.shard_map(
        body,
        mesh=mesh,
        in_specs=(
            P(None, None, "gx", "gy", None),
            P(None, None, None, "gx", "gy", None),
            P(None, "gx", "gy", None),
            P(("gx", "gy"), None),
            P(("gx", "gy")),
            P(("gx", "gy")),
            P(None, ("gx", "gy")),
        ),
        out_specs=P(None, None, "gx", "gy", None),
        check_vma=False,
    )
```

profile of v0, /device:TPU:0, one launch (start us, length us, event | category | flops | bytes accessed | tf_op | source)
XLA Modules:
  0.0 84.2 jit_solution(6107799063079017723)
XLA Ops:
  0.0 0.7 fusion.23
  0.7 0.7 or_select_fusion
  1.5 0.7 mul.157
  2.2 0.1 mul.161
  2.3 0.8 broadcast_multiply_fusion.1
  3.1 0.5 broadcast.280
  3.6 1.4 %reduce.3 = s32[2048]{0:T(1024)S(1)} reduce(s32[2048,1]{0,1:T(1,128)} %param.16, s32[]{:T(128)} %broadcast.280), dimensions={1}, to_apply=%param.16.reduce_sub_computation.3 | reduce | bytes 16388 | tf_op args[3]
  5.0 0.1 convert_reduce_fusion
  5.2 0.8 multiply_reduce_fusion
  6.0 1.1 %fusion.3 = f32[8,256]{1,0:T(8,128)S(1)} fusion(bf16[256,256,1]{1,0,2:T(8,128)(2,1)} %constant.105, f32[32,8]{1,0:T(8,128)S(1)} %copy.20, s32[8,256]{1,0:T(8,128)S(1)} %eq.75), kind=kOutput, calls=%fused_computation.4 | convolution fusion | flops 34011136 | bytes 148480 | tf_op jit(solution)/shard_map/nbr,rs->nbs/dot_general | solution.py:318
  7.2 0.7 add_select_fusion
  7.9 0.8 stack.21
  8.7 0.1 mul.160
  8.9 0.1 mul.171
  9.0 0.8 reduce-precision_convert_fusion.1
  9.8 0.7 fusion.10
  10.6 0.7 fusion
  11.3 0.1 copy.25
  11.4 0.7 fusion.17
  12.2 0.6 pad_maximum_fusion.1.asked_ref
  12.8 0.8 %multiply_divide_fusion.dim_ref = f32[8,64,128]{2,1,0:T(8,128)} fusion(f32[64,128]{1,0:T(8,128)S(1)} %broadcast_bitcast_fusion, f32[8,64]{1,0:T(8,128)S(1)} %mul.171), kind=kLoop, calls=%fused_computation.16 | loop fusion | flops 131072 | bytes 296960 | tf_op jit(solution)/shard_map/div | solution.py:364
  13.7 0.8 broadcast_in_dim.12.wm_ref
  14.5 67.2 %advance.1 = f32[2,8,64,128]{3,2,1,0:T(8,128)} custom-call(f32[2,8,64,128]{3,2,1,0:T(8,128)} %bitcast.27, f32[3,2,8,64,128]{4,3,2,1,0:T(8,128)} %bitcast.29, f32[2,128]{1,0:T(2,128)} %bitcast.40, f32[8,64,128]{2,1,0:T(8,128)} %broadcast_in_dim.12.wm_ref, f32[8,64,128]{2,1,0:T(8,128)} %multiply_divide_fusion.dim_ref, ...), custom_call_target="tpu_custom_call" | custom-call | tf_op jit(solution)/shard_map/advance/pallas_call | solution.py:368
  81.7 2.6 %multiply_add_fusion = f32[2,512,1,1,128]{4,3,2,1,0:T(1,128)} fusion(f32[2,512,1,1,128]{4,3,2,1,0:T(1,128)} %bitcast.28, f32[2,512,1,1,128]{4,3,2,1,0:T(1,128)S(1)} %copy-done), kind=kLoop, calls=%fused_computation.10 | loop fusion | flops 262144 | bytes 1572864 | tf_op jit(solution)/shard_map/add | solution.py:402
  (19 shorter events, 0.5 us)
Async XLA Ops:
  14.5 67.2 %copy-start = (f32[2,512,1,1,128]{4,3,2,1,0:T(1,128)S(1)}, f32[2,512,1,1,128]{4,3,2,1,0:T(1,128)}, u32[]{:S(2)}) copy-start(f32[2,512,1,1,128]{4,3,2,1,0:T(1,128)} %param.13) | copy-start | bytes 1572868
where the time goes:
time: 84.7 us; the launch traced here: 84.2 us
  Pallas kernels  67.2 us (79%)
  other arithmetic  11.6 us (14%)
  local copies, waits for them, and re-layouts  3.48 us (4%)
  matrix products  1.82 us (2%)
    pallas_call x1, Pallas kernels, body(): pl.pallas_call(functools.partial(step_kernel, derivative, gll_nodes), out...  67.2 us
    add x1, other arithmetic, body(): return scalar / 3.0 + out.reshape(scalar.shape)  2.56 us

commit v1 on v0

v1 whole, which is shorter than its diff:
```python
import functools
import jax
import jax.numpy as jnp
import numpy as np
from jax import lax
from jax.experimental import pallas as pl
from jax.experimental.pallas import tpu as pltpu
from jax.sharding import PartitionSpec as P

time_step = 0.01
penalty_rate = 50.0
volume_factor = 0.125
node_inner = [0.8717401485096066, 0.5917001814331423, 0.20929921790247888]


def legendre_seven(point):
    before, current = (1.0, point)
    for order in range(1, 7):
        before, current = (
            current,
            ((2 * order + 1) * point * current - order * before) / (order + 1),
        )
    return current


def gll_tables():
    degree = 7
    gll_nodes = [-1.0] + [-v for v in node_inner] + node_inner[::-1] + [1.0]
    end_values = [legendre_seven(v) for v in gll_nodes]
    weights = [2.0 / (degree * (degree + 1) * v * v) for v in end_values]
    derivative = [[0.0] * 8 for _ in range(8)]
    for a in range(8):
        for b in range(8):
            if a != b:
                derivative[a][b] = end_values[a] / (end_values[b] * (gll_nodes[a] - gll_nodes[b]))
    derivative[0][0] = -degree * (degree + 1) / 4.0
    derivative[7][7] = degree * (degree + 1) / 4.0
    return (gll_nodes, weights, derivative)


MESH = pl.DeviceIdType.MESH
HEADINGS = [(-1, 0), (1, 0), (0, -1), (0, 1), (-1, -1), (-1, 1), (1, -1), (1, 1)]


def halves(value):
    high = value.astype(jnp.bfloat16)
    return high, (value - high.astype(jnp.float32)).astype(jnp.bfloat16)


def mm(a, b):
    return jnp.dot(a, b, preferred_element_type=jnp.float32)


def mm_t(a, b):
    return lax.dot_general(a, b, (((1,), (1,)), ((), ())), preferred_element_type=jnp.float32)


def mm3(op_high, op_low, value):
    high, low = halves(value)
    return mm(op_high, high) + mm(op_high, low) + mm(op_low, high)


def step_kernel(
    tables, owner_ref, elem_ref, point_ref, coord_ref, nu_ref, start_hbm, vel_hbm, ops_hbm,
    out_ref,
    start, vel, ops, cur, local, work, grad, wm, dim, held,
    hot_s, within_s, rank_s, asked, got, pick, basis_ref, spread_q, spread_e,
    ans, rep, hx, hy, he,
    in_sem, ask_send, ask_recv, ans_send, ans_recv, halo_send, halo_recv,
):
    gll_nodes, weights, derivative = tables
    f32, bf, i32 = jnp.float32, jnp.bfloat16, jnp.int32
    gx, gy = lax.axis_index("gx"), lax.axis_index("gy")
    nx, ny = lax.axis_size("gx"), lax.axis_size("gy")
    n = nx * ny
    me = gx * ny + gy
    ez = start.shape[-1]
    rows = owner_ref.shape[-1]
    cap = ans.shape[-1]
    groups, _, lanes = pick.shape
    per = lanes // cap
    width = within_s.shape[-1]
    blocks = rows // width
    half_rows = rows // 2

    barrier = pltpu.get_barrier_semaphore()

    def place(d):
        return (d // ny, lax.rem(d, ny))

    def greet(step, carry):
        d = lax.rem(me + step, n)
        pl.semaphore_signal(barrier, inc=1, device_id=place(d), device_id_type=MESH)
        return carry

    lax.fori_loop(1, n, greet, 0)
    loads = [
        pltpu.make_async_copy(start_hbm, start, in_sem.at[0]),
        pltpu.make_async_copy(vel_hbm, vel, in_sem.at[1]),
        pltpu.make_async_copy(ops_hbm, ops, in_sem.at[2]),
    ]
    for load in loads:
        load.start()

    for b in range(blocks):
        spot = slice(b * width, (b + 1) * width)
        iota_n = lax.broadcasted_iota(i32, (n, width), 0)
        hot_s[b * n:(b + 1) * n, :] = jnp.where(owner_ref[0:1, spot] == iota_n, 1.0, 0.0).astype(bf)
    first_of = lax.broadcasted_iota(i32, (width, width), 0)
    second_of = lax.broadcasted_iota(i32, (width, width), 1)
    earlier = jnp.where(first_of < second_of, 1.0, 0.0).astype(bf)
    within_s[...] = mm(hot_s[...], earlier)
    sums = mm(hot_s[...], jnp.ones((width, 128), bf))
    offset = jnp.zeros((n, 128), f32)
    inverse = jnp.zeros((2 * n, 128), f32)
    lane_f = lax.broadcasted_iota(i32, (n, width), 1).astype(f32)
    slot_iota = lax.broadcasted_iota(i32, (128, width), 0)
    for b in range(blocks):
        spot = slice(b * width, (b + 1) * width)
        mine = hot_s[b * n:(b + 1) * n, :].astype(f32)
        wide_offset = jnp.concatenate([offset] * (width // 128), axis=1)
        place_in = (within_s[b * n:(b + 1) * n, :] + wide_offset) * mine
        rank = jnp.sum(place_in, axis=0, keepdims=True).astype(i32)
        rank_s[0:1, spot] = rank
        slot_hot = jnp.where(slot_iota == rank, 1.0, 0.0).astype(bf)
        named = jnp.concatenate([mine * lane_f, mine * float(b)], axis=0).astype(bf)
        inverse = inverse + mm_t(named, slot_hot)
        offset = offset + sums[b * n:(b + 1) * n, :]
    source = (inverse[0:n] + float(width) * inverse[n:2 * n]).astype(i32)
    tile_of, lane_of = source // 128, lax.rem(source, 128)
    found = [jnp.zeros((n, 128), f32) for _ in range(4)]
    for t in range(rows // 128):
        spot = slice(t * 128, (t + 1) * 128)
        here = tile_of == t
        for c in range(4):
            row = coord_ref[c:c + 1, spot] if c < 3 else elem_ref[0:1, spot].astype(f32)
            picked = jnp.take_along_axis(jnp.broadcast_to(row, (n, 128)), lane_of, axis=1)
            found[c] = jnp.where(here, picked, found[c])
    found[3] = found[3] + jnp.where(source < half_rows, float(ez), 0.0)
    for c in range(4):
        for d in range(n):
            asked[d, c:c + 1, :] = found[c][d:d + 1, 0:cap]

    pl.semaphore_wait(barrier, n - 1)

    def ask(step, carry):
        d = lax.rem(me + n // 2 + step, n)

        @pl.when(d != me)
        def _():
            pltpu.make_async_remote_copy(
                src_ref=asked.at[d], dst_ref=got.at[me], send_sem=ask_send, recv_sem=ask_recv,
                device_id=place(d), device_id_type=MESH,
            ).start()

        return carry

    lax.fori_loop(0, n, ask, 0)

    k_iota = lax.broadcasted_iota(i32, (8, ez), 0)
    e_iota = lax.broadcasted_iota(i32, (8, ez), 1)
    w_k = jnp.zeros((8, ez), f32)
    for k in range(8):
        w_k = jnp.where(k_iota == k, volume_factor * weights[k], w_k)
    joined = ((k_iota == 0) & (e_iota > 0)) | ((k_iota == 7) & (e_iota < ez - 1))
    inv_k = time_step / jnp.where(joined, 2.0 * w_k, w_k)
    inv_x = [1.0 / v for v in weights]
    inv_y = [1.0 / v for v in weights]
    inv_x[0] = jnp.where(gx > 0, 0.5, 1.0) * inv_x[0]
    inv_x[7] = jnp.where(gx < nx - 1, 0.5, 1.0) * inv_x[7]
    inv_y[0] = jnp.where(gy > 0, 0.5, 1.0) * inv_y[0]
    inv_y[7] = jnp.where(gy < ny - 1, 0.5, 1.0) * inv_y[7]
    for i in range(8):
        for j in range(8):
            wm[i, 8 * j:8 * j + 8, :] = (weights[i] * weights[j]) * w_k
            dim[i, 8 * j:8 * j + 8, :] = (inv_x[i] * inv_y[j]) * inv_k

    part = 256
    for m in range(2):
        for b in range(half_rows // part):
            spot = slice(m * half_rows + b * part, m * half_rows + (b + 1) * part)
            to = slice(b * part, (b + 1) * part)
            point = point_ref[0:1, spot]
            tall = lax.broadcasted_iota(i32, (512, part), 0)
            short = lax.broadcasted_iota(i32, (ez, part), 0)
            spread_q[m, :, to] = jnp.where(tall == point // ez, 1.0, 0.0).astype(bf)
            spread_e[m, :, to] = jnp.where(short == lax.rem(point, ez), 1.0, 0.0).astype(bf)
        held[m] = mm_t(spread_q[m], spread_e[m]).reshape(8, 64, ez)
        for i in range(8):
            held[m, i] = held[m, i] * (penalty_rate * wm[i])

    for load in loads:
        load.wait()

    def halo_copy(s, m, number):
        dx, dy = HEADINGS[number]
        lines = pl.ds(0 if dy < 0 else 56, 8)
        plane = 0 if dx < 0 else 7
        if dy == 0:
            source, target = local.at[m, plane], hx.at[s, number, m]
        elif dx == 0:
            source, target = local.at[m, :, lines, :], hy.at[s, number - 2, m]
        else:
            source, target = local.at[m, plane, lines, :], he.at[s, number - 4, m]
        return pltpu.make_async_remote_copy(
            src_ref=source, dst_ref=target, send_sem=halo_send.at[s, m, number], recv_sem=halo_recv.at[s, m, number],
            device_id=(gx + dx, gy + dy), device_id_type=MESH,
        )

    def inside(dx, dy):
        return (gx + dx >= 0) & (gx + dx < nx) & (gy + dy >= 0) & (gy + dy < ny)

    def operators(value):
        for m in range(2):
            lo = slice(m * ez, (m + 1) * ez)
            scale = nu_ref[m:m + 1, :]
            for half in range(2):
                some = slice(4 * half, 4 * half + 4)
                part = value[m, some].reshape(256, ez)
                grad[0, some, :, lo] = mm3(ops[0], ops[1], part).reshape(4, 64, ez)
                grad[1, some, :, lo] = mm3(ops[2], ops[3], part).reshape(4, 64, ez)
            for a in range(8):
                gxa = (2.0 * derivative[a][0]) * value[m, 0]
                for i in range(1, 8):
                    gxa = gxa + (2.0 * derivative[a][i]) * value[m, i]
                wma = wm[a]
                gya = grad[0, a, :, lo]
                gza = grad[1, a, :, lo]
                adv = vel[0, m, a] * gxa + vel[1, m, a] * gya + vel[2, m, a] * gza
                local[m, a] = -(wma * adv) - held[m, a] * value[m, a]
                wn = wma * scale
                work[m, a] = wn * gxa
                grad[0, a, :, lo] = wn * gya
                grad[1, a, :, lo] = wn * gza
            for half in range(2):
                some = slice(4 * half, 4 * half + 4)
                part_y = grad[0, some, :, lo].reshape(256, ez)
                part_z = grad[1, some, :, lo].reshape(256, ez)
                back = mm3(ops[4], ops[5], part_y) + mm3(ops[6], ops[7], part_z)
                local[m, some] -= back.reshape(4, 64, ez)
            for i in range(8):
                total = (2.0 * derivative[0][i]) * work[m, 0]
                for a in range(1, 8):
                    total = total + (2.0 * derivative[a][i]) * work[m, a]
                local[m, i] -= total

    operators(start)
    pltpu.make_async_copy(asked.at[me], got.at[me], in_sem.at[0]).start()
    pltpu.make_async_copy(asked.at[me], got.at[me], in_sem.at[0]).wait()
    others = got.at[pl.ds(0, n - 1)]
    pltpu.make_async_copy(others, others, ask_recv).wait()

    def prepare(g):
        wanted = jnp.concatenate([got[g * per + t] for t in range(per)], axis=1)
        wide = lax.broadcasted_iota(i32, (2 * ez, lanes), 0)
        pick[g] = jnp.where(wide == wanted[3:4].astype(i32), 1.0, 0.0).astype(bf)
        away = [wanted - v for v in gll_nodes]
        before = [None, away[0]]
        for k in range(1, 7):
            before.append(before[-1] * away[k])
        after = [None] * 7 + [None]
        after[6] = away[7]
        for k in range(5, -1, -1):
            after[k] = after[k + 1] * away[k + 1]
        for j in range(8):
            norm = 1.0
            for k in range(8):
                if k != j:
                    norm *= gll_nodes[j] - gll_nodes[k]
            factor = after[0] if j == 0 else before[7] if j == 7 else before[j] * after[j]
            factor = factor * (1.0 / norm)
            for c in range(3):
                basis_ref[g, 8 * c + j:8 * c + j + 1, :] = factor[c:c + 1]

    for s in range(3):
        value = start if s == 0 else cur
        both = jnp.concatenate([value[0].reshape(512, ez), value[1].reshape(512, ez)], axis=1)
        high, low = halves(both)

        def interpolate(p, carry):
            off = groups // 2 + ((p + 1) // 2) * (1 - 2 * lax.rem(p, 2))
            g = lax.rem(me // per + off + groups, groups)
            if s == 0:
                prepare(g)
            found = mm(high, pick[g]) + mm(low, pick[g])
            acc = found[0:64] * basis_ref[g, 0:1, :]
            for i in range(1, 8):
                acc = acc + found[64 * i:64 * i + 64] * basis_ref[g, i:i + 1, :]
            acc2 = acc[0:8] * basis_ref[g, 8:9, :]
            for j in range(1, 8):
                acc2 = acc2 + acc[8 * j:8 * j + 8] * basis_ref[g, 8 + j:9 + j, :]
            row = jnp.sum(acc2 * basis_ref[g, 16:24, :], axis=0, keepdims=True)
            for t in range(per):
                ans[s, g * per + t] = row[:, t * cap:(t + 1) * cap]
            for t in range(per):
                d = g * per + t

                @pl.when(d != me)
                def _(d=d):
                    pltpu.make_async_remote_copy(
                        src_ref=ans.at[s, d], dst_ref=rep.at[s, me],
                        send_sem=ans_send.at[s], recv_sem=ans_recv.at[s],
                        device_id=place(d), device_id_type=MESH,
                    ).start()

            return carry

        lax.fori_loop(0, groups, interpolate, 0)
        if s > 0:
            operators(cur)
        rep[s, me] = ans[s, me]
        arrived = ans.at[s, pl.ds(0, n - 1)]
        pltpu.make_async_copy(arrived, arrived, ans_recv.at[s]).wait()

        answers = jnp.concatenate([rep[s, d] for d in range(n)], axis=0)
        if cap < 128:
            answers = jnp.concatenate([answers, jnp.zeros((n, 128 - cap), f32)], axis=1)
        for m in range(2):
            pieces = []
            for t in range(half_rows // 128):
                spot = slice(m * half_rows + t * 128, m * half_rows + (t + 1) * 128)
                slot = jnp.broadcast_to(rank_s[0:1, spot], (n, 128))
                taken = jnp.take_along_axis(answers, slot, axis=1)
                own = owner_ref[0:1, spot] == lax.broadcasted_iota(i32, (n, 128), 0)
                pieces.append(jnp.sum(jnp.where(own, taken, 0.0), axis=0, keepdims=True))
            row_high, row_low = halves(jnp.concatenate(pieces, axis=1))
            where_e = spread_e[m]
            spread_v = jnp.concatenate([where_e * row_high, where_e * row_low], axis=0)
            added = mm_t(spread_q[m], spread_v)
            for i in range(8):
                rows_i = slice(64 * i, 64 * i + 64)
                local[m, i] += (penalty_rate * wm[i]) * (added[rows_i, :ez] + added[rows_i, ez:])
            lane = lax.broadcasted_iota(i32, (8, ez), 1)
            for i in range(8):
                lower = local[m, i, pl.ds(0, 8, stride=8), :]
                upper = local[m, i, pl.ds(7, 8, stride=8), :]
                shared = upper + pltpu.roll(lower, ez - 1, 1)
                local[m, i, pl.ds(7, 8, stride=8), :] = jnp.where(lane < ez - 1, shared, upper)
                local[m, i, pl.ds(0, 8, stride=8), :] = jnp.where(lane > 0, pltpu.roll(shared, 1, 1), lower)
            for number, (dx, dy) in enumerate(HEADINGS):
                @pl.when(inside(dx, dy))
                def _(m=m, number=number):
                    halo_copy(s, m, number).start()

        target = cur if s < 2 else out_ref
        share = (1.0, 0.25, 2.0 / 3.0)[s]
        for m in range(2):
            for i in range(8):
                moved = value[m, i] + local[m, i] * dim[i]
                if s == 0:
                    cur[m, i] = moved
                elif s == 1:
                    cur[m, i] = 0.75 * start[m, i] + 0.25 * moved
                else:
                    out_ref[m, i] = start[m, i] * (1.0 / 3.0) + (2.0 / 3.0) * moved
        for m in range(2):
            for number, (dx, dy) in enumerate(HEADINGS):
                @pl.when(inside(-dx, -dy))
                def _(m=m, number=number, dx=dx, dy=dy):
                    halo_copy(s, m, number).wait_recv()
                    plane = 7 if dx < 0 else 0
                    lines = slice(56, 64) if dy < 0 else slice(0, 8)
                    if dy == 0:
                        target[m, plane] += hx[s, number, m] * (share * dim[plane])
                    elif dx == 0:
                        target[m, :, lines, :] += hy[s, number - 2, m] * (share * dim[:, lines, :])
                    else:
                        target[m, plane, lines, :] += he[s, number - 4, m] * (share * dim[plane, lines, :])
        for m in range(2):
            for number, (dx, dy) in enumerate(HEADINGS):
                @pl.when(inside(dx, dy))
                def _(m=m, number=number):
                    halo_copy(s, m, number).wait_send()

    sent = got.at[pl.ds(0, n - 1)]
    pltpu.make_async_copy(sent, sent, ask_send).wait()
    for s in range(3):
        whole = ans.at[s, pl.ds(0, n - 1)]
        pltpu.make_async_copy(whole, whole, ans_send.at[s]).wait()


def split_host(matrix):
    high = matrix.astype(jnp.bfloat16)
    low = (matrix - high.astype(np.float64)).astype(jnp.bfloat16)
    return [high, low]


def body(scalar, velocity, diffusivity, recv_owner, donor_elem, recv_point, recv_coords):
    tables = gll_tables()
    derivative = tables[2]
    ez = scalar.shape[4]
    n = lax.axis_size("gx") * lax.axis_size("gy")
    rows = recv_owner.shape[0]
    cap = max(2, 2 * rows // n)
    per = max(1, min(n, 512 // cap))
    groups, lanes = n // per, per * cap
    width = min(256, rows)
    blocks = rows // width
    bf, f32, i32 = jnp.bfloat16, jnp.float32, jnp.int32

    half_eye = np.eye(4)
    table = 2.0 * np.asarray(derivative, np.float64)
    along_y = np.kron(half_eye, np.kron(table, np.eye(8)))
    along_z = np.kron(half_eye, np.kron(np.eye(8), table))
    ops = []
    for matrix in (along_y, along_z, along_y.T, along_z.T):
        ops = ops + split_host(matrix)
    ops = jnp.asarray(np.stack(ops))

    vmem = pltpu.VMEM
    dma = pltpu.SemaphoreType.DMA
    field = (2, 8, 64, ez)
    in_vmem, anywhere = pl.BlockSpec(memory_space=vmem), pl.BlockSpec(memory_space=pl.ANY)
    out = pl.pallas_call(
        functools.partial(step_kernel, tables),
        out_shape=jax.ShapeDtypeStruct(field, f32),
        in_specs=[in_vmem] * 5 + [anywhere] * 3,
        out_specs=in_vmem,
        scratch_shapes=[
            vmem(field, f32),
            vmem((3,) + field, f32),
            vmem((8, 256, 256), bf),
            vmem(field, f32),
            vmem(field, f32),
            vmem(field, f32),
            vmem((2, 8, 64, 2 * ez), f32),
            vmem((8, 64, ez), f32),
            vmem((8, 64, ez), f32),
            vmem(field, f32),
            vmem((blocks * n, width), bf),
            vmem((blocks * n, width), f32),
            vmem((1, rows), i32),
            vmem((n, 4, cap), f32),
            vmem((n, 4, cap), f32),
            vmem((groups, 2 * ez, lanes), bf),
            vmem((groups, 24, lanes), f32),
            vmem((2, 512, rows // 2), bf),
            vmem((2, ez, rows // 2), bf),
            vmem((3, n, 1, cap), f32),
            vmem((3, n, 1, cap), f32),
            vmem((3, 2, 2, 64, ez), f32),
            vmem((3, 2, 2, 8, 8, ez), f32),
            vmem((3, 4, 2, 8, ez), f32),
            dma((3,)),
            dma,
            dma,
            dma((3,)),
            dma((3,)),
            dma((3, 2, 8)),
            dma((3, 2, 8)),
        ],
        compiler_params=pltpu.CompilerParams(collective_id=0, has_side_effects=True),
        name="advance",
    )(
        recv_owner.reshape(1, rows), donor_elem.reshape(1, rows), recv_point.reshape(1, rows), recv_coords,
        diffusivity.reshape(2, ez), scalar.reshape(field), velocity.reshape((3,) + field), ops,
    )
    return out.reshape(scalar.shape)


def solution(mesh):
    return jax.shard_map(
        body,
        mesh=mesh,
        in_specs=(
            P(None, None, "gx", "gy", None),
            P(None, None, None, "gx", "gy", None),
            P(None, "gx", "gy", None),
            P(("gx", "gy"), None),
            P(("gx", "gy")),
            P(("gx", "gy")),
            P(None, ("gx", "gy")),
        ),
        out_specs=P(None, None, "gx", "gy", None),
        check_vma=False,
    )
```

time: 84.7 us -> 53.7 us (0.63)
  Pallas kernels: 67.2 us -> 51.6 us
  other arithmetic: 11.6 us -> 0 us
  matrix products: 1.82 us -> 0 us
  local copies, waits for them, and re-layouts: 3.48 us -> 1.87 us
    pallas_call x1, Pallas kernels: 67.2 us -> 51.6 us  [body(): pl.pallas_call(functools.partial(step_kernel, tables), out_shape=jax.Shap...]
    add x2 -> x0, other arithmetic: 2.59 us -> none  [the longest x1 2.56 us: body(): return scalar / 3.0 + out.reshape(scalar.shape)]
    dot_general x2 -> x0, matrix products: 1.82 us -> none  [the longest x1 1.11 us: body(): jnp.einsum('nbr,rs->nbs', hot3, earlier, preferred_element_type=f32)]
    mul x4 -> x0, other arithmetic: 1.56 us -> none  [the longest x1 0.8 us: gll_tables(): weight_row[:, None, None] * weight_row[None, :, None]]
    select_n x2 -> x0, other arithmetic: 1.46 us -> none  [the longest x1 0.74 us: body(): mass_z = jnp.where(joined_z, shared[:, None], single[:, None])]
    convert_element_type x3 -> x0, other arithmetic: 1.43 us -> none  [the longest x1 0.72 us: body(): (owners[None, :] == jnp.arange(n, dtype=jnp.int32)[:, None]).astype(bf)]
    unnamed x2 -> x0, other arithmetic: 1.37 us -> none
    unnamed x4 -> x1, local copies, waits for them, and re-layouts: 0.52 us -> 1.87 us
where the time goes in v1:
time: 53.7 us; the launch traced here: 53.5 us
  Pallas kernels  51.6 us (96%)
  local copies, waits for them, and re-layouts  1.87 us (3%)
    pallas_call x1, Pallas kernels, body(): pl.pallas_call(functools.partial(step_kernel, tables), out_shape=jax.Shap...  51.6 us
    unnamed x1, local copies, waits for them, and re-layouts  1.87 us

profile of v1, /device:TPU:0, one launch (start us, length us, event | category | flops | bytes accessed | tf_op | source)
XLA Modules:
  0.0 53.5 jit_solution(3553161623225925912)
XLA Ops:
  0.0 51.6 %advance.1 = f32[2,8,64,128]{3,2,1,0:T(8,128)} custom-call(s32[1,2048]{1,0:T(1,128)} %bitcast.12, s32[1,2048]{1,0:T(1,128)} %bitcast.13, s32[1,2048]{1,0:T(1,128)} %bitcast.14, f32[3,2048]{1,0:T(4,128)} %coord_ref.1, f32[2,128]{1,0:T(2,128)} %bitcast.15, f32[2,8,64,128]{3,2,1,0:T(8,128)} %bitcast.11, f32[3,2,8,64,128]{4,3,2,1,0:T(8,128)} %bitcast.10, ...), custom_call_target="tpu_custom_call" | custom-call | tf_op jit(solution)/shard_map/advance/pallas_call | solution.py:414
  51.6 1.9 %copy.11 = f32[2,512,1,1,128]{4,3,2,1,0:T(1,128)} copy(f32[2,512,1,1,128]{4,3,2,1,0:T(1,128)} %bitcast.9) | data formatting | bytes 1048576

commit v2 on v1

--- a/solution.py
+++ b/solution.py
@@ -40,6 +40,9 @@
 
 MESH = pl.DeviceIdType.MESH
 HEADINGS = [(-1, 0), (1, 0), (0, -1), (0, 1), (-1, -1), (-1, 1), (1, -1), (1, 1)]
+INNER = range(1, 7)
+FACE = [(i, j) for i in (0, 7) for j in range(8)] + [(i, j) for j in (0, 7) for i in INNER]
+INTERIOR = [(i, j) for i in INNER for j in INNER]
 
 
 def halves(value):
@@ -65,7 +68,7 @@
     out_ref,
     start, vel, ops, cur, local, work, grad, wm, dim, held,
     hot_s, within_s, rank_s, asked, got, pick, basis_ref, spread_q, spread_e,
-    ans, rep, hx, hy, he,
+    ans, rep, hx, hy, he, lhs_face, lhs_inner, inner_part,
     in_sem, ask_send, ask_recv, ans_send, ans_recv, halo_send, halo_recv,
 ):
     gll_nodes, weights, derivative = tables
@@ -88,12 +91,16 @@
     def place(d):
         return (d // ny, lax.rem(d, ny))
 
-    def greet(step, carry):
-        d = lax.rem(me + step, n)
-        pl.semaphore_signal(barrier, inc=1, device_id=place(d), device_id_type=MESH)
+    def greet(a, carry):
+        px = lax.rem(gx + nx // 2 + a, nx)
+        for b in range(ny):
+            @pl.when((px != gx) | (gy != b))
+            def _(b=b):
+                pl.semaphore_signal(barrier, inc=1, device_id=(px, b), device_id_type=MESH)
+
         return carry
 
-    lax.fori_loop(1, n, greet, 0)
+    lax.fori_loop(0, nx, greet, 0)
     loads = [
         pltpu.make_async_copy(start_hbm, start, in_sem.at[0]),
         pltpu.make_async_copy(vel_hbm, vel, in_sem.at[1]),
@@ -143,19 +150,22 @@
 
     pl.semaphore_wait(barrier, n - 1)
 
-    def ask(step, carry):
-        d = lax.rem(me + n // 2 + step, n)
-
-        @pl.when(d != me)
-        def _():
-            pltpu.make_async_remote_copy(
-                src_ref=asked.at[d], dst_ref=got.at[me], send_sem=ask_send, recv_sem=ask_recv,
-                device_id=place(d), device_id_type=MESH,
-            ).start()
+    own_group = me // per
+
+    def ask(a, carry):
+        px = lax.rem(gx + nx // 2 + a, nx)
+        for b in range(ny):
+            @pl.when((px != gx) | (gy != b))
+            def _(b=b):
+                pltpu.make_async_remote_copy(
+                    src_ref=asked.at[px * ny + b], dst_ref=got.at[me],
+                    send_sem=ask_send, recv_sem=ask_recv.at[own_group],
+                    device_id=(px, b), device_id_type=MESH,
+                ).start()
 
         return carry
 
-    lax.fori_loop(0, n, ask, 0)
+    lax.fori_loop(0, nx, ask, 0)
 
     k_iota = lax.broadcasted_iota(i32, (8, ez), 0)
     e_iota = lax.broadcasted_iota(i32, (8, ez), 1)
@@ -181,13 +191,15 @@
             spot = slice(m * half_rows + b * part, m * half_rows + (b + 1) * part)
             to = slice(b * part, (b + 1) * part)
             point = point_ref[0:1, spot]
-            tall = lax.broadcasted_iota(i32, (512, part), 0)
+            eight = lax.broadcasted_iota(i32, (8, part), 0)
+            tall = jnp.concatenate([eight + (64 * i + 8 * j) for i, j in FACE + INTERIOR], axis=0)
             short = lax.broadcasted_iota(i32, (ez, part), 0)
             spread_q[m, :, to] = jnp.where(tall == point // ez, 1.0, 0.0).astype(bf)
             spread_e[m, :, to] = jnp.where(short == lax.rem(point, ez), 1.0, 0.0).astype(bf)
-        held[m] = mm_t(spread_q[m], spread_e[m]).reshape(8, 64, ez)
-        for i in range(8):
-            held[m, i] = held[m, i] * (penalty_rate * wm[i])
+        count = mm_t(spread_q[m], spread_e[m])
+        for at, (i, j) in enumerate(FACE + INTERIOR):
+            spot = slice(8 * j, 8 * j + 8)
+            held[m, i, spot] = count[8 * at:8 * at + 8] * (penalty_rate * wm[i, spot])
 
     for load in loads:
         load.wait()
@@ -247,9 +259,6 @@
     operators(start)
     pltpu.make_async_copy(asked.at[me], got.at[me], in_sem.at[0]).start()
     pltpu.make_async_copy(asked.at[me], got.at[me], in_sem.at[0]).wait()
-    others = got.at[pl.ds(0, n - 1)]
-    pltpu.make_async_copy(others, others, ask_recv).wait()
-
     def prepare(g):
         wanted = jnp.concatenate([got[g * per + t] for t in range(per)], axis=1)
         wide = lax.broadcasted_iota(i32, (2 * ez, lanes), 0)
@@ -272,24 +281,62 @@
             for c in range(3):
                 basis_ref[g, 8 * c + j:8 * c + j + 1, :] = factor[c:c + 1]
 
+    nearby = got.at[pl.ds(0, per - 1)]
+    pltpu.make_async_copy(nearby, nearby, ask_recv.at[own_group]).wait()
+    prepare(own_group)
+
+    def next_group(p, carry):
+        off = ((p + 1) // 2) * (1 - 2 * lax.rem(p, 2))
+        g = lax.rem(own_group + off + groups, groups)
+        some = got.at[pl.ds(0, per)]
+        pltpu.make_async_copy(some, some, ask_recv.at[g]).wait()
+        prepare(g)
+        return carry
+
+    lax.fori_loop(1, groups, next_group, 0)
+
+    def split_lines(value, lines, into):
+        both = jnp.concatenate(
+            [jnp.concatenate([value[m, i, 8 * j:8 * j + 8] for i, j in lines], axis=0) for m in range(2)], axis=1
+        )
+        into[0], into[1] = halves(both)
+
+    def contract(lines, lhs, g):
+        found = mm(lhs[0], pick[g]) + mm(lhs[1], pick[g])
+        total = None
+        for j in range(8):
+            line = None
+            for at, (i, jj) in enumerate(lines):
+                if jj == j:
+                    term = found[8 * at:8 * at + 8] * basis_ref[g, i:i + 1, :]
+                    line = term if line is None else line + term
+            if line is not None:
+                line = line * basis_ref[g, 8 + j:9 + j, :]
+                total = line if total is None else total + line
+        return total
+
+    def sum_third(flat, m, first, size, stride):
+        lane = lax.broadcasted_iota(i32, (size, ez), 1)
+        low_rows, high_rows = pl.ds(first, size, stride=stride), pl.ds(first + 7, size, stride=stride)
+        lower, upper = flat[m, low_rows, :], flat[m, high_rows, :]
+        shared = upper + pltpu.roll(lower, ez - 1, 1)
+        flat[m, high_rows, :] = jnp.where(lane < ez - 1, shared, upper)
+        flat[m, low_rows, :] = jnp.where(lane > 0, pltpu.roll(shared, 1, 1), lower)
+
+    flat = local.reshape(2, 512, ez)
+
     for s in range(3):
         value = start if s == 0 else cur
-        both = jnp.concatenate([value[0].reshape(512, ez), value[1].reshape(512, ez)], axis=1)
-        high, low = halves(both)
+        if s == 0:
+            split_lines(start, INTERIOR, lhs_inner)
+        split_lines(value, FACE, lhs_face)
 
         def interpolate(p, carry):
             off = groups // 2 + ((p + 1) // 2) * (1 - 2 * lax.rem(p, 2))
-            g = lax.rem(me // per + off + groups, groups)
-            if s == 0:
-                prepare(g)
-            found = mm(high, pick[g]) + mm(low, pick[g])
-            acc = found[0:64] * basis_ref[g, 0:1, :]
-            for i in range(1, 8):
-                acc = acc + found[64 * i:64 * i + 64] * basis_ref[g, i:i + 1, :]
-            acc2 = acc[0:8] * basis_ref[g, 8:9, :]
-            for j in range(1, 8):
-                acc2 = acc2 + acc[8 * j:8 * j + 8] * basis_ref[g, 8 + j:9 + j, :]
-            row = jnp.sum(acc2 * basis_ref[g, 16:24, :], axis=0, keepdims=True)
+            g = lax.rem(own_group + off + groups, groups)
+            total = contract(FACE, lhs_face, g)
+            total = total + (contract(INTERIOR, lhs_inner, g) if s == 0 else inner_part[g])
+            row = jnp.sum(total * basis_ref[g, 16:24, :], axis=0, keepdims=True)
             for t in range(per):
                 ans[s, g * per + t] = row[:, t * cap:(t + 1) * cap]
             for t in range(per):
@@ -315,6 +362,14 @@
         answers = jnp.concatenate([rep[s, d] for d in range(n)], axis=0)
         if cap < 128:
             answers = jnp.concatenate([answers, jnp.zeros((n, 128 - cap), f32)], axis=1)
+
+        def scatter(m, lines, first):
+            added = mm_t(spread_q[m, first:first + 8 * len(lines), :], spread_v[m])
+            for at, (i, j) in enumerate(lines):
+                spot, rows_at = slice(8 * j, 8 * j + 8), slice(8 * at, 8 * at + 8)
+                local[m, i, spot] += (penalty_rate * wm[i, spot]) * (added[rows_at, :ez] + added[rows_at, ez:])
+
+        spread_v = []
         for m in range(2):
             pieces = []
             for t in range(half_rows // 128):
@@ -325,18 +380,12 @@
                 pieces.append(jnp.sum(jnp.where(own, taken, 0.0), axis=0, keepdims=True))
             row_high, row_low = halves(jnp.concatenate(pieces, axis=1))
             where_e = spread_e[m]
-            spread_v = jnp.concatenate([where_e * row_high, where_e * row_low], axis=0)
-            added = mm_t(spread_q[m], spread_v)
-            for i in range(8):
-                rows_i = slice(64 * i, 64 * i + 64)
-                local[m, i] += (penalty_rate * wm[i]) * (added[rows_i, :ez] + added[rows_i, ez:])
-            lane = lax.broadcasted_iota(i32, (8, ez), 1)
-            for i in range(8):
-                lower = local[m, i, pl.ds(0, 8, stride=8), :]
-                upper = local[m, i, pl.ds(7, 8, stride=8), :]
-                shared = upper + pltpu.roll(lower, ez - 1, 1)
-                local[m, i, pl.ds(7, 8, stride=8), :] = jnp.where(lane < ez - 1, shared, upper)
-                local[m, i, pl.ds(0, 8, stride=8), :] = jnp.where(lane > 0, pltpu.roll(shared, 1, 1), lower)
+            spread_v.append(jnp.concatenate([where_e * row_high, where_e * row_low], axis=0))
+            scatter(m, FACE, 0)
+            for i in (0, 7):
+                sum_third(flat, m, 64 * i + 8, 6, 8)
+            for j in (0, 7):
+                sum_third(flat, m, 8 * j, 8, 64)
             for number, (dx, dy) in enumerate(HEADINGS):
                 @pl.when(inside(dx, dy))
                 def _(m=m, number=number):
@@ -345,6 +394,9 @@
         target = cur if s < 2 else out_ref
         share = (1.0, 0.25, 2.0 / 3.0)[s]
         for m in range(2):
+            scatter(m, INTERIOR, 8 * len(FACE))
+            for i in INNER:
+                sum_third(flat, m, 64 * i + 8, 6, 8)
             for i in range(8):
                 moved = value[m, i] + local[m, i] * dim[i]
                 if s == 0:
@@ -353,6 +405,14 @@
                     cur[m, i] = 0.75 * start[m, i] + 0.25 * moved
                 else:
                     out_ref[m, i] = start[m, i] * (1.0 / 3.0) + (2.0 / 3.0) * moved
+        if s < 2:
+            split_lines(cur, INTERIOR, lhs_inner)
+
+            def ahead(g, carry):
+                inner_part[g] = contract(INTERIOR, lhs_inner, g)
+                return carry
+
+            lax.fori_loop(0, groups, ahead, 0)
         for m in range(2):
             for number, (dx, dy) in enumerate(HEADINGS):
                 @pl.when(inside(-dx, -dy))
@@ -441,9 +501,12 @@
             vmem((3, 2, 2, 64, ez), f32),
             vmem((3, 2, 2, 8, 8, ez), f32),
             vmem((3, 4, 2, 8, ez), f32),
+            vmem((2, 8 * len(FACE), 2 * ez), bf),
+            vmem((2, 8 * len(INTERIOR), 2 * ez), bf),
+            vmem((groups, 8, lanes), f32),
             dma((3,)),
             dma,
-            dma,
+            dma((groups,)),
             dma((3,)),
             dma((3,)),
             dma((3, 2, 8)),

time: 53.7 us -> 50.7 us (0.944)
  Pallas kernels: 51.6 us -> 48.6 us
    pallas_call x1, Pallas kernels: 51.6 us -> 48.6 us  [body(): pl.pallas_call(functools.partial(step_kernel, tables), out_shape=jax.Shap...]
where the time goes in v2:
time: 50.7 us; the launch traced here: 50.5 us
  Pallas kernels  48.6 us (96%)
  local copies, waits for them, and re-layouts  1.87 us (4%)
    pallas_call x1, Pallas kernels, body(): pl.pallas_call(functools.partial(step_kernel, tables), out_shape=jax.Shap...  48.6 us
    unnamed x1, local copies, waits for them, and re-layouts  1.87 us

profile of v2, /device:TPU:0, one launch (start us, length us, event | category | flops | bytes accessed | tf_op | source)
XLA Modules:
  0.0 50.5 jit_solution(2244990194582590164)
XLA Ops:
  0.0 48.6 %advance.1 = f32[2,8,64,128]{3,2,1,0:T(8,128)} custom-call(s32[1,2048]{1,0:T(1,128)} %bitcast.12, s32[1,2048]{1,0:T(1,128)} %bitcast.13, s32[1,2048]{1,0:T(1,128)} %bitcast.14, f32[3,2048]{1,0:T(4,128)} %coord_ref.1, f32[2,128]{1,0:T(2,128)} %bitcast.15, f32[2,8,64,128]{3,2,1,0:T(8,128)} %bitcast.11, f32[3,2,8,64,128]{4,3,2,1,0:T(8,128)} %bitcast.10, ...), custom_call_target="tpu_custom_call" | custom-call | tf_op jit(solution)/shard_map/advance/pallas_call | solution.py:474
  48.6 1.9 %copy.11 = f32[2,512,1,1,128]{4,3,2,1,0:T(1,128)} copy(f32[2,512,1,1,128]{4,3,2,1,0:T(1,128)} %bitcast.9) | data formatting | bytes 1048576

commit v3 on v2

--- a/solution.py
+++ b/solution.py
@@ -68,7 +68,7 @@
     out_ref,
     start, vel, ops, cur, local, work, grad, wm, dim, held,
     hot_s, within_s, rank_s, asked, got, pick, basis_ref, spread_q, spread_e,
-    ans, rep, hx, hy, he, lhs_face, lhs_inner, inner_part,
+    ans, rep, hx, hy, he, lhs, inner_part,
     in_sem, ask_send, ask_recv, ans_send, ans_recv, halo_send, halo_recv,
 ):
     gll_nodes, weights, derivative = tables
@@ -281,28 +281,16 @@
             for c in range(3):
                 basis_ref[g, 8 * c + j:8 * c + j + 1, :] = factor[c:c + 1]
 
-    nearby = got.at[pl.ds(0, per - 1)]
-    pltpu.make_async_copy(nearby, nearby, ask_recv.at[own_group]).wait()
-    prepare(own_group)
-
-    def next_group(p, carry):
-        off = ((p + 1) // 2) * (1 - 2 * lax.rem(p, 2))
-        g = lax.rem(own_group + off + groups, groups)
-        some = got.at[pl.ds(0, per)]
-        pltpu.make_async_copy(some, some, ask_recv.at[g]).wait()
-        prepare(g)
-        return carry
-
-    lax.fori_loop(1, groups, next_group, 0)
-
     def split_lines(value, lines, into):
         both = jnp.concatenate(
             [jnp.concatenate([value[m, i, 8 * j:8 * j + 8] for i, j in lines], axis=0) for m in range(2)], axis=1
         )
-        into[0], into[1] = halves(both)
-
-    def contract(lines, lhs, g):
-        found = mm(lhs[0], pick[g]) + mm(lhs[1], pick[g])
+        lhs[0, into, :], lhs[1, into, :] = halves(both)
+
+    face_at, inner_at = slice(0, 8 * len(FACE)), slice(8 * len(FACE), 512)
+
+    def contract(lines, at_rows, g):
+        found = mm(lhs[0, at_rows], pick[g]) + mm(lhs[1, at_rows], pick[g])
         total = None
         for j in range(8):
             line = None
@@ -325,17 +313,22 @@
 
     flat = local.reshape(2, 512, ez)
 
+    def halo_sent(s):
+        for m in range(2):
+            for number, (dx, dy) in enumerate(HEADINGS):
+                @pl.when(inside(dx, dy))
+                def _(m=m, number=number):
+                    halo_copy(s, m, number).wait_send()
+
     for s in range(3):
         value = start if s == 0 else cur
-        if s == 0:
-            split_lines(start, INTERIOR, lhs_inner)
-        split_lines(value, FACE, lhs_face)
-
-        def interpolate(p, carry):
-            off = groups // 2 + ((p + 1) // 2) * (1 - 2 * lax.rem(p, 2))
-            g = lax.rem(own_group + off + groups, groups)
-            total = contract(FACE, lhs_face, g)
-            total = total + (contract(INTERIOR, lhs_inner, g) if s == 0 else inner_part[g])
+        split_lines(value, FACE, face_at)
+
+        def interpolate(g):
+            if s == 0:
+                total = contract(FACE + INTERIOR, slice(0, 512), g)
+            else:
+                total = contract(FACE, face_at, g) + inner_part[g]
             row = jnp.sum(total * basis_ref[g, 16:24, :], axis=0, keepdims=True)
             for t in range(per):
                 ans[s, g * per + t] = row[:, t * cap:(t + 1) * cap]
@@ -350,9 +343,38 @@
                         device_id=place(d), device_id_type=MESH,
                     ).start()
 
+        def from_afar(p, carry):
+            off = groups // 2 + ((p + 1) // 2) * (1 - 2 * lax.rem(p, 2))
+            interpolate(lax.rem(own_group + off + groups, groups))
             return carry
 
-        lax.fori_loop(0, groups, interpolate, 0)
+        def request(p, carry):
+            off = ((p + 1) // 2) * (1 - 2 * lax.rem(p, 2))
+            g = lax.rem(own_group + off + groups, groups)
+            some = got.at[pl.ds(0, per)]
+            pltpu.make_async_copy(some, some, ask_recv.at[g]).wait()
+            prepare(g)
+            return carry
+
+        if s == 0:
+            split_lines(value, INTERIOR, inner_at)
+            nearby = got.at[pl.ds(0, per - 1)]
+            pltpu.make_async_copy(nearby, nearby, ask_recv.at[own_group]).wait()
+            prepare(own_group)
+            early = 2
+
+            def soon(p, carry):
+                interpolate(lax.rem(own_group - p + groups, groups))
+                return carry
+
+            if early > 1:
+                lax.fori_loop(1, early, request, 0)
+            lax.fori_loop(0, early, soon, 0)
+            lax.fori_loop(max(early, 1), groups, request, 0)
+            lax.fori_loop(0, groups - early, from_afar, 0)
+        else:
+            lax.fori_loop(0, groups, from_afar, 0)
+            halo_sent(s - 1)
         if s > 0:
             operators(cur)
         rep[s, me] = ans[s, me]
@@ -406,10 +428,10 @@
                 else:
                     out_ref[m, i] = start[m, i] * (1.0 / 3.0) + (2.0 / 3.0) * moved
         if s < 2:
-            split_lines(cur, INTERIOR, lhs_inner)
+            split_lines(cur, INTERIOR, inner_at)
 
             def ahead(g, carry):
-                inner_part[g] = contract(INTERIOR, lhs_inner, g)
+                inner_part[g] = contract(INTERIOR, inner_at, g)
                 return carry
 
             lax.fori_loop(0, groups, ahead, 0)
@@ -426,12 +448,7 @@
                         target[m, :, lines, :] += hy[s, number - 2, m] * (share * dim[:, lines, :])
                     else:
                         target[m, plane, lines, :] += he[s, number - 4, m] * (share * dim[plane, lines, :])
-        for m in range(2):
-            for number, (dx, dy) in enumerate(HEADINGS):
-                @pl.when(inside(dx, dy))
-                def _(m=m, number=number):
-                    halo_copy(s, m, number).wait_send()
-
+    halo_sent(2)
     sent = got.at[pl.ds(0, n - 1)]
     pltpu.make_async_copy(sent, sent, ask_send).wait()
     for s in range(3):
@@ -470,7 +487,7 @@
     vmem = pltpu.VMEM
     dma = pltpu.SemaphoreType.DMA
     field = (2, 8, 64, ez)
-    in_vmem, anywhere = pl.BlockSpec(memory_space=vmem), pl.BlockSpec(memory_space=pl.ANY)
+    in_vmem, anywhere = pl.BlockSpec(memory_space=vmem), pl.BlockSpec(memory_space=pltpu.HBM)
     out = pl.pallas_call(
         functools.partial(step_kernel, tables),
         out_shape=jax.ShapeDtypeStruct(field, f32),
@@ -501,8 +518,7 @@
             vmem((3, 2, 2, 64, ez), f32),
             vmem((3, 2, 2, 8, 8, ez), f32),
             vmem((3, 4, 2, 8, ez), f32),
-            vmem((2, 8 * len(FACE), 2 * ez), bf),
-            vmem((2, 8 * len(INTERIOR), 2 * ez), bf),
+            vmem((2, 512, 2 * ez), bf),
             vmem((groups, 8, lanes), f32),
             dma((3,)),
             dma,
@@ -512,11 +528,13 @@
             dma((3, 2, 8)),
             dma((3, 2, 8)),
         ],
-        compiler_params=pltpu.CompilerParams(collective_id=0, has_side_effects=True),
+        compiler_params=pltpu.CompilerParams(collective_id=0, has_side_effects=True, vmem_limit_bytes=44 * 1024 * 1024),
         name="advance",
     )(
-        recv_owner.reshape(1, rows), donor_elem.reshape(1, rows), recv_point.reshape(1, rows), recv_coords,
-        diffusivity.reshape(2, ez), scalar.reshape(field), velocity.reshape((3,) + field), ops,
+        *[pltpu.with_memory_space_constraint(v, pltpu.HBM) for v in (
+            recv_owner.reshape(1, rows), donor_elem.reshape(1, rows), recv_point.reshape(1, rows), recv_coords,
+            diffusivity.reshape(2, ez), scalar.reshape(field), velocity.reshape((3,) + field), ops,
+        )]
     )
     return out.reshape(scalar.shape)
 

time: 50.7 us -> 48.7 us (0.961)
  local copies, waits for them, and re-layouts: 1.87 us -> 0.8 us
  Pallas kernels: 48.6 us -> 47.7 us
    unnamed x1, local copies, waits for them, and re-layouts: 1.87 us -> 0.8 us
    pallas_call x1, Pallas kernels: 48.6 us -> 47.7 us  [body(): pl.pallas_call(functools.partial(step_kernel, tables), out_shape=jax.Shap...]
where the time goes in v3:
time: 48.7 us; the launch traced here: 48.5 us
  Pallas kernels  47.7 us (98%)
  local copies, waits for them, and re-layouts  0.8 us (2%)
    pallas_call x1, Pallas kernels, body(): pl.pallas_call(functools.partial(step_kernel, tables), out_shape=jax.Shap...  47.7 us

profile of v3, /device:TPU:0, one launch (start us, length us, event | category | flops | bytes accessed | tf_op | source)
XLA Modules:
  0.0 48.5 jit_solution(2338518356585433506)
XLA Ops:
  0.0 47.7 %advance.1 = f32[2,8,64,128]{3,2,1,0:T(8,128)S(1)} custom-call(s32[1,2048]{1,0:T(1,128)} %bitcast.12, s32[1,2048]{1,0:T(1,128)} %bitcast.13, s32[1,2048]{1,0:T(1,128)} %bitcast.14, f32[3,2048]{1,0:T(4,128)} %coord_ref.1, f32[2,128]{1,0:T(2,128)} %bitcast.15, f32[2,8,64,128]{3,2,1,0:T(8,128)} %bitcast.11, f32[3,2,8,64,128]{4,3,2,1,0:T(8,128)} %bitcast.10, ...), custom_call_target="tpu_custom_call" | custom-call | tf_op jit(solution)/shard_map/advance/pallas_call | solution.py:491
  47.7 0.8 %copy.11 = f32[2,512,1,1,128]{4,3,2,1,0:T(1,128)} copy(f32[2,512,1,1,128]{4,3,2,1,0:T(1,128)S(1)} %bitcast.9) | data formatting | bytes 1048576

commit v4 on v3

--- a/solution.py
+++ b/solution.py
@@ -373,7 +373,7 @@
             lax.fori_loop(max(early, 1), groups, request, 0)
             lax.fori_loop(0, groups - early, from_afar, 0)
         else:
-            lax.fori_loop(0, groups, from_afar, 0)
+            lax.fori_loop(0, groups, from_afar, 0, unroll=2)
             halo_sent(s - 1)
         if s > 0:
             operators(cur)
@@ -434,7 +434,7 @@
                 inner_part[g] = contract(INTERIOR, inner_at, g)
                 return carry
 
-            lax.fori_loop(0, groups, ahead, 0)
+            lax.fori_loop(0, groups, ahead, 0, unroll=2)
         for m in range(2):
             for number, (dx, dy) in enumerate(HEADINGS):
                 @pl.when(inside(-dx, -dy))

time: 48.7 us -> 48.2 us (0.990)
  Pallas kernels: 47.7 us -> 47.2 us
    pallas_call x1, Pallas kernels: 47.7 us -> 47.2 us  [body(): pl.pallas_call(functools.partial(step_kernel, tables), out_shape=jax.Shap...]
where the time goes in v4:
time: 48.2 us; the launch traced here: 48 us
  Pallas kernels  47.2 us (98%)
  local copies, waits for them, and re-layouts  0.8 us (2%)
    pallas_call x1, Pallas kernels, body(): pl.pallas_call(functools.partial(step_kernel, tables), out_shape=jax.Shap...  47.2 us

profile of v4, /device:TPU:0, one launch (start us, length us, event | category | flops | bytes accessed | tf_op | source)
XLA Modules:
  0.0 48.0 jit_solution(6957816978667687687)
XLA Ops:
  0.0 47.2 %advance.1 = f32[2,8,64,128]{3,2,1,0:T(8,128)S(1)} custom-call(s32[1,2048]{1,0:T(1,128)} %bitcast.12, s32[1,2048]{1,0:T(1,128)} %bitcast.13, s32[1,2048]{1,0:T(1,128)} %bitcast.14, f32[3,2048]{1,0:T(4,128)} %coord_ref.1, f32[2,128]{1,0:T(2,128)} %bitcast.15, f32[2,8,64,128]{3,2,1,0:T(8,128)} %bitcast.11, f32[3,2,8,64,128]{4,3,2,1,0:T(8,128)} %bitcast.10, ...), custom_call_target="tpu_custom_call" | custom-call | tf_op jit(solution)/shard_map/advance/pallas_call | solution.py:491
  47.2 0.8 %copy.11 = f32[2,512,1,1,128]{4,3,2,1,0:T(1,128)} copy(f32[2,512,1,1,128]{4,3,2,1,0:T(1,128)S(1)} %bitcast.9) | data formatting | bytes 1048576

commit v5 on v4

--- a/solution.py
+++ b/solution.py
@@ -371,7 +371,7 @@
                 lax.fori_loop(1, early, request, 0)
             lax.fori_loop(0, early, soon, 0)
             lax.fori_loop(max(early, 1), groups, request, 0)
-            lax.fori_loop(0, groups - early, from_afar, 0)
+            lax.fori_loop(0, groups - early, from_afar, 0, unroll=2)
         else:
             lax.fori_loop(0, groups, from_afar, 0, unroll=2)
             halo_sent(s - 1)

time: 48.2 us -> 48.1 us (level)
  no operation moved by 1% of the time
where the time goes in v5:
time: 48.1 us; the launch traced here: 47.9 us
  Pallas kernels  47.1 us (98%)
  local copies, waits for them, and re-layouts  0.8 us (2%)
    pallas_call x1, Pallas kernels, body(): pl.pallas_call(functools.partial(step_kernel, tables), out_shape=jax.Shap...  47.1 us

profile of v5, /device:TPU:0, one launch (start us, length us, event | category | flops | bytes accessed | tf_op | source)
XLA Modules:
  0.0 47.9 jit_solution(16255197842851443282)
XLA Ops:
  0.0 47.1 %advance.1 = f32[2,8,64,128]{3,2,1,0:T(8,128)S(1)} custom-call(s32[1,2048]{1,0:T(1,128)} %bitcast.12, s32[1,2048]{1,0:T(1,128)} %bitcast.13, s32[1,2048]{1,0:T(1,128)} %bitcast.14, f32[3,2048]{1,0:T(4,128)} %coord_ref.1, f32[2,128]{1,0:T(2,128)} %bitcast.15, f32[2,8,64,128]{3,2,1,0:T(8,128)} %bitcast.11, f32[3,2,8,64,128]{4,3,2,1,0:T(8,128)} %bitcast.10, ...), custom_call_target="tpu_custom_call" | custom-call | tf_op jit(solution)/shard_map/advance/pallas_call | solution.py:491
  47.2 0.8 %copy.11 = f32[2,512,1,1,128]{4,3,2,1,0:T(1,128)} copy(f32[2,512,1,1,128]{4,3,2,1,0:T(1,128)S(1)} %bitcast.9) | data formatting | bytes 1048576
